TPU v7x, 32 devices: a whole 2x2x4 slice. The times are simulated.
32 devices in a mesh: dp: 8 (over y, x, core), tensor: 4 (over z).
Axes of the slice: x: 2, y: 2, z: 4, core: 2. Of those that a mesh axis runs over, the one named last changes fastest.
Arguments:
- block_input: bfloat16 [8192, 2048], P('dp'), may hold values from -24 to 24
- segments: int32 [8192], P('dp'), may hold values from 0 to 15, never falling along the last dimension, each value on 1 to 2048 neighbouring positions
- norm_gain: bfloat16 [2048], P('dp'), may hold values from 0.5 to 1.5
- norm_bias: bfloat16 [2048], P('dp'), may hold values from -1.75 to 1.75
- qkv_weight: bfloat16 [2048, 3, 2048], P('dp', None, 'tensor'), may hold values from -1 to 1
- query_value_bias: bfloat16 [2, 32, 64], P(None, 'tensor', 'dp'), may hold values from -1.75 to 1.75
- key_bias: bfloat16 [32, 32], P('tensor', 'dp'), may hold values from -3 to 3
- dense_weight: bfloat16 [2048, 2048], P('tensor', 'dp'), may hold values from -1.5 to 1.5
- dense_bias: bfloat16 [2048], P('dp'), may hold values from -1.75 to 1.75
- up_weight: bfloat16 [2048, 8192], P('dp', 'tensor'), may hold values from -0.125 to 0.125
- up_bias: bfloat16 [128, 64], P('tensor', 'dp'), may hold values from -1.75 to 1.75
- down_weight: bfloat16 [8192, 2048], P('tensor', 'dp'), may hold values from -0.0625 to 0.0625
- down_bias: bfloat16 [2048], P('dp'), may hold values from -1.75 to 1.75
- cotangent: bfloat16 [8192, 2048], P('dp'), may hold values from -8 to 8
Outputs:
- block_output: bfloat16 [8192, 2048], P('dp')
- input_grad: float32 [8192, 2048], P('dp')
- norm_gain_grad: float32 [2048], P('dp')
- norm_bias_grad: float32 [2048], P('dp')
- qkv_weight_grad: float32 [2048, 3, 2048], P('dp', None, 'tensor')
- query_value_bias_grad: float32 [2, 32, 64], P(None, 'tensor', 'dp')
- key_bias_grad: float32 [32, 32], P('tensor', 'dp')
- dense_weight_grad: float32 [2048, 2048], P('tensor', 'dp')
- dense_bias_grad: float32 [2048], P('dp')
- up_weight_grad: float32 [2048, 8192], P('dp', 'tensor')
- up_bias_grad: float32 [128, 64], P('tensor', 'dp')
- down_weight_grad: float32 [8192, 2048], P('tensor', 'dp')
- down_bias_grad: float32 [2048], P('dp')
Inputs may be any that keep to these rules, and one draw needn't show every extreme that they name: `segments`: segment numbers never fall along the tokens; each segment has 1 to 2048 tokens, one exactly 2048.
All inputs are finite; a program needn't handle non-finite values.
Results may differ from a plain program's by a relative error of at most 0.015.
The roundings to bfloat16 on the way count: a program that leaves them out, or rounds other values in their place, can miss the bound.
Values may be sent and summed in bfloat16 or wider, within the bound.
A program may use at most 256 MiB of HBM per device.

v0:
```python
import math
import jax
import jax.numpy as jnp
from jax import lax
from jax.sharding import PartitionSpec as P

HEAD = 64
ROT = 32
SEQ = 512
EPSILON = 1e-05
SCALE = 0.125
NEGATIVE = -1e30


def rotary_tables(seg_rows):
    seq_len = seg_rows.shape[1]
    position = jnp.arange(seq_len, dtype=jnp.int32)
    starting = jnp.concatenate(
        [jnp.ones((seg_rows.shape[0], 1), dtype=jnp.bool_), seg_rows[:, 1:] != seg_rows[:, :-1]],
        axis=1,
    )
    starts = lax.cummax(jnp.where(starting, position[None, :], jnp.int32(0)), axis=1)
    offset = (position[None, :] - starts).astype(jnp.float32)
    halfway = ROT // 2
    inverse = 10000.0 ** (-(jnp.arange(halfway, dtype=jnp.float32) * (2.0 / ROT)))
    angles = offset[:, :, None] * inverse
    return (jnp.cos(angles), jnp.sin(angles))


def rotate(tensor, cosine_table, sine_table, direction):
    halfway = ROT // 2
    leading = tensor[..., :halfway]
    trailing = tensor[..., halfway:ROT]
    others = tensor[..., ROT:]
    cosine_part = cosine_table[:, :, None, :]
    sine_part = sine_table[:, :, None, :] * direction
    return jnp.concatenate(
        [
            leading * cosine_part - trailing * sine_part,
            trailing * cosine_part + leading * sine_part,
            others,
        ],
        axis=-1,
    )


def allowed_pairs(seg_rows):
    seq_len = seg_rows.shape[1]
    position = jnp.arange(seq_len, dtype=jnp.int32)
    causal = position[:, None] >= position[None, :]
    same_doc = seg_rows[:, :, None] == seg_rows[:, None, :]
    return (same_doc & causal[None])[:, None]


def gelu_tanh(inputs):
    return jax.nn.gelu(inputs, approximate=True)


def masked_scores(queries, key_rows, allowed):
    scores = (
        jnp.einsum("nqhd,nkhd->nhqk", queries, key_rows, preferred_element_type=jnp.float32) * SCALE
    )
    return jnp.where(allowed, scores, NEGATIVE)


def attend_group(placeholder, inputs):
    queries, key_rows, values, allowed = inputs
    scores = masked_scores(queries, key_rows, allowed)
    row_max = jnp.max(scores, axis=-1, keepdims=True)
    row_total = jnp.sum(jnp.exp(scores - row_max), axis=-1, keepdims=True)
    log_total = row_max + jnp.log(row_total)
    prob_low = jnp.exp(scores - log_total).astype(jnp.bfloat16)
    mixed_part = jnp.einsum(
        "nhqk,nkhd->nqhd", prob_low, values, preferred_element_type=jnp.float32
    ).astype(jnp.bfloat16)
    return (placeholder, (mixed_part, log_total))


def attend_back_group(placeholder, inputs):
    queries, key_rows, values, allowed, log_total, grad_mixed = inputs
    scores = masked_scores(queries, key_rows, allowed)
    probabilities = jnp.exp(scores - log_total)
    prob_low = probabilities.astype(jnp.bfloat16)
    grad_values = jnp.einsum(
        "nhqk,nqhd->nkhd", prob_low, grad_mixed, preferred_element_type=jnp.float32
    )
    grad_probs = jnp.einsum(
        "nqhd,nkhd->nhqk", grad_mixed, values, preferred_element_type=jnp.float32
    )
    row_delta = jnp.sum(probabilities * grad_probs, axis=-1, keepdims=True)
    grad_scores = (probabilities * (grad_probs - row_delta) * SCALE).astype(jnp.bfloat16)
    grad_queries = jnp.einsum(
        "nhqk,nkhd->nqhd", grad_scores, key_rows, preferred_element_type=jnp.float32
    )
    grad_keys = jnp.einsum(
        "nhqk,nqhd->nkhd", grad_scores, queries, preferred_element_type=jnp.float32
    )
    return (placeholder, (grad_queries, grad_keys, grad_values))


def local(
    block_input,
    segments,
    norm_gain,
    norm_bias,
    qkv_weight,
    query_value_bias,
    key_bias,
    dense_weight,
    dense_bias,
    up_weight,
    up_bias,
    down_weight,
    down_bias,
    cotangent,
):
    gathered = (
        lax.all_gather(norm_gain, "dp", axis=0, tiled=True),
        lax.all_gather(norm_bias, "dp", axis=0, tiled=True),
        lax.all_gather(qkv_weight, "dp", axis=0, tiled=True),
        lax.all_gather(query_value_bias, "dp", axis=2, tiled=True),
        lax.all_gather(key_bias, "dp", axis=1, tiled=True),
        lax.all_gather(dense_weight, "dp", axis=1, tiled=True),
        lax.all_gather(dense_bias, "dp", axis=0, tiled=True),
        lax.all_gather(up_weight, "dp", axis=0, tiled=True),
        lax.all_gather(up_bias, "dp", axis=1, tiled=True),
        lax.all_gather(down_weight, "dp", axis=1, tiled=True),
        lax.all_gather(down_bias, "dp", axis=0, tiled=True),
    )
    (
        gain_all,
        shift_all,
        qkv_all,
        qv_all,
        key_all,
        dense_all,
        dense_shift_all,
        up_all,
        up_shift_all,
        down_all,
        down_shift_all,
    ) = gathered
    row_count, model_width = block_input.shape
    local_width = qkv_all.shape[2]
    heads_here = local_width // HEAD
    seqs_here = row_count // SEQ
    per_step = math.gcd(seqs_here, max(1, 512 // SEQ))
    groups = seqs_here // per_step

    def to_groups(tensor):
        return tensor.reshape((groups, per_step) + tensor.shape[1:])

    def from_groups(tensor):
        return tensor.reshape((seqs_here,) + tensor.shape[2:])

    widened = block_input.astype(jnp.float32)
    row_mean = jnp.mean(widened, axis=1, keepdims=True)
    centred = widened - row_mean
    row_var = jnp.mean(centred * centred, axis=1, keepdims=True)
    inv_std = lax.rsqrt(row_var + EPSILON)
    normed = centred * inv_std
    normed_low = (normed * gain_all.astype(jnp.float32) + shift_all.astype(jnp.float32)).astype(
        jnp.bfloat16
    )
    qkv_flat = qkv_all.reshape(model_width, 3 * local_width)
    projected = jnp.dot(normed_low, qkv_flat, preferred_element_type=jnp.float32).reshape(
        seqs_here, SEQ, 3, heads_here, HEAD
    )
    seq_segs = segments.reshape(seqs_here, SEQ)
    cosine_table, sine_table = rotary_tables(seq_segs)
    allowed = allowed_pairs(seq_segs)
    qv_wide = qv_all.astype(jnp.float32)
    key_full = jnp.concatenate(
        [key_all.astype(jnp.float32), jnp.zeros((heads_here, HEAD - ROT), jnp.float32)], axis=1
    )
    queries = rotate(projected[:, :, 0] + qv_wide[0], cosine_table, sine_table, 1.0).astype(
        jnp.bfloat16
    )
    key_rows = rotate(projected[:, :, 1] + key_full, cosine_table, sine_table, 1.0).astype(
        jnp.bfloat16
    )
    values = (projected[:, :, 2] + qv_wide[1]).astype(jnp.bfloat16)
    placeholder = jnp.zeros((), jnp.float32)
    group_inputs = (to_groups(queries), to_groups(key_rows), to_groups(values), to_groups(allowed))
    unused, (mixed_groups, log_groups) = lax.scan(attend_group, placeholder, group_inputs)
    mixed_rows = mixed_groups.reshape(row_count, local_width)
    hidden = jnp.dot(normed_low, up_all, preferred_element_type=jnp.float32) + up_shift_all.reshape(
        -1
    ).astype(jnp.float32)
    activated = gelu_tanh(hidden).astype(jnp.bfloat16)
    branches = jnp.dot(mixed_rows, dense_all, preferred_element_type=jnp.float32) + jnp.dot(
        activated, down_all, preferred_element_type=jnp.float32
    )
    dense_shift = dense_shift_all.astype(jnp.float32)
    down_shift = down_shift_all.astype(jnp.float32)
    summed_out = lax.psum(branches, "tensor")
    block_output = (widened + summed_out + dense_shift + down_shift).astype(jnp.bfloat16)
    gain_back, qkv_back, dense_back, up_back, down_back = (
        lax.all_gather(norm_gain, "dp", axis=0, tiled=True),
        lax.all_gather(qkv_weight, "dp", axis=0, tiled=True),
        lax.all_gather(dense_weight, "dp", axis=1, tiled=True),
        lax.all_gather(up_weight, "dp", axis=0, tiled=True),
        lax.all_gather(down_weight, "dp", axis=1, tiled=True),
    )
    grad_wide = cotangent.astype(jnp.float32)
    grad_bias_out = jnp.sum(grad_wide, axis=0)
    grad_dense = jnp.dot(mixed_rows.T, cotangent, preferred_element_type=jnp.float32)
    grad_down = jnp.dot(activated.T, cotangent, preferred_element_type=jnp.float32)
    grad_mixed = (
        jnp.dot(cotangent, dense_back.T, preferred_element_type=jnp.float32)
        .astype(jnp.bfloat16)
        .reshape(seqs_here, SEQ, heads_here, HEAD)
    )
    grad_act = jnp.dot(cotangent, down_back.T, preferred_element_type=jnp.float32)
    grad_hidden = jax.vjp(gelu_tanh, hidden)[1](grad_act)[0]
    grad_up_bias = jnp.sum(grad_hidden, axis=0).reshape(up_shift_all.shape)
    grad_hidden_low = grad_hidden.astype(jnp.bfloat16)
    grad_up = jnp.dot(normed_low.T, grad_hidden_low, preferred_element_type=jnp.float32)
    back_inputs = group_inputs + (log_groups, to_groups(grad_mixed))
    unused_back, (query_groups, key_groups, value_groups) = lax.scan(
        attend_back_group, placeholder, back_inputs
    )
    grad_queries = rotate(from_groups(query_groups), cosine_table, sine_table, -1.0)
    grad_keys = rotate(from_groups(key_groups), cosine_table, sine_table, -1.0)
    grad_values = from_groups(value_groups)
    grad_qv = jnp.stack([jnp.sum(grad_queries, axis=(0, 1)), jnp.sum(grad_values, axis=(0, 1))])
    grad_key_bias = jnp.sum(grad_keys[..., :ROT], axis=(0, 1))
    grad_projected = (
        jnp.stack([grad_queries, grad_keys, grad_values], axis=2)
        .reshape(row_count, 3 * local_width)
        .astype(jnp.bfloat16)
    )
    grad_qkv = jnp.dot(normed_low.T, grad_projected, preferred_element_type=jnp.float32).reshape(
        model_width, 3, local_width
    )
    grad_normed_part = jnp.dot(
        grad_projected,
        qkv_back.reshape(model_width, 3 * local_width).T,
        preferred_element_type=jnp.float32,
    ) + jnp.dot(grad_hidden_low, up_back.T, preferred_element_type=jnp.float32)
    grad_normed = lax.psum(grad_normed_part.astype(jnp.bfloat16), "tensor").astype(jnp.float32)
    grad_gain = jnp.sum(grad_normed * normed, axis=0)
    grad_shift = jnp.sum(grad_normed, axis=0)
    scaled = grad_normed * gain_back.astype(jnp.float32)
    input_grad = (
        inv_std
        * (
            scaled
            - jnp.mean(scaled, axis=1, keepdims=True)
            - normed * jnp.mean(scaled * normed, axis=1, keepdims=True)
        )
        + grad_wide
    )
    summed = (
        lax.psum_scatter(grad_gain, "dp", scatter_dimension=0, tiled=True),
        lax.psum_scatter(grad_shift, "dp", scatter_dimension=0, tiled=True),
        lax.psum_scatter(grad_qkv, "dp", scatter_dimension=0, tiled=True),
        lax.psum_scatter(grad_qv, "dp", scatter_dimension=2, tiled=True),
        lax.psum_scatter(grad_key_bias, "dp", scatter_dimension=1, tiled=True),
        lax.psum_scatter(grad_dense, "dp", scatter_dimension=1, tiled=True),
        lax.psum_scatter(grad_bias_out, "dp", scatter_dimension=0, tiled=True),
        lax.psum_scatter(grad_up, "dp", scatter_dimension=0, tiled=True),
        lax.psum_scatter(grad_up_bias, "dp", scatter_dimension=1, tiled=True),
        lax.psum_scatter(grad_down, "dp", scatter_dimension=1, tiled=True),
    )
    return (
        block_output,
        input_grad,
        summed[0],
        summed[1],
        summed[2],
        summed[3],
        summed[4],
        summed[5],
        summed[6],
        summed[7],
        summed[8],
        summed[9],
        summed[6],
    )


def solution(mesh):
    in_specs = (
        P("dp", None),
        P("dp"),
        P("dp"),
        P("dp"),
        P("dp", None, "tensor"),
        P(None, "tensor", "dp"),
        P("tensor", "dp"),
        P("tensor", "dp"),
        P("dp"),
        P("dp", "tensor"),
        P("tensor", "dp"),
        P("tensor", "dp"),
        P("dp"),
        P("dp", None),
    )
    out_specs = (
        P("dp", None),
        P("dp", None),
        P("dp"),
        P("dp"),
        P("dp", None, "tensor"),
        P(None, "tensor", "dp"),
        P("tensor", "dp"),
        P("tensor", "dp"),
        P("dp"),
        P("dp", "tensor"),
        P("tensor", "dp"),
        P("tensor", "dp"),
        P("dp"),
    )
    return jax.shard_map(local, mesh=mesh, in_specs=in_specs, out_specs=out_specs, check_vma=False)
```

profile of v0, /device:TPU:0, one launch (start us, length us, event | category | flops | bytes accessed | tf_op | source)
XLA Modules:
  0.0 1116.1 jit_solution(14657728340286387230)
XLA Ops:
  22.3 10.4 all-gather.1
  32.7 9.1 all-gather
  41.8 8.0 all-gather.2
  49.8 9.2 all_gather.45
  59.8 8.6 all_gather.41
  74.7 6.2 convolution_convert_fusion
  89.3 10.1 fusion.146
  101.6 13.5 %while.26 = (s32[]{:T(128)}, bf16[2,1,512,8,64]{2,4,3,1,0:T(8,128)(2,1)}, f32[2,1,8,512,1]{3,2,4,1,0:T(8,128)S(1)}, bf16[2,1,512,8,64]{2,4,3,1,0:T(8,128)(2,1)},...) while((s32[]{:T(128)}, ...), condition=%wide.region_7.8_spmd, body=%wide.region_4.7_spmd.sunk | while | flops 560197632 | bytes 41289912 | solution.py:185
  115.0 85.6 %while.27 = (s32[]{:T(128)}, f32[2,1,512,8,64]{2,4,3,1,0:T(8,128)}, f32[2,1,512,8,64]{2,4,3,1,0:T(8,128)}, f32[2,1,512,8,64]{2,4,3,1,0:T(8,128)}, bf16[2,1,512,8...) while((s32[]{:T(128)}, f32[2,1,512,8,64]{2,4,3,1,0:T(8,128)}, ...), condition=%wide.region_11.12_spmd, body=%wide.region_9.11_spmd.sunk | while | flops 1396712448 | bytes 159765776 | solution.py:220
  128.5 14.5 %fusion.204 = f32[2,1,512,8,64]{2,4,3,1,0:T(8,128)} fusion(f32[2,1,512,8,64]{2,4,3,1,0:T(8,128)} %get-tuple-element.472, s32[]{:T(128)S(6)} %copy.169, f32[8,512,512]{1,2,0:T(8,128)} %fusion.201, f32[8,512,512]{1,2,0:T(8,128)} %copy-done, f32[8,512]{1,0:T(8,128)S(1)} %dynamic-slice_bitcast_fusion.7, ...), kind=kOutput, calls=%fused_computation.46.clone.1 | convolution fusion | flops 291508736 | bytes 35685376 | tf_op jit(solution)/shard_map/while/body/eval_jaxpr/nhqk,nqhd->nkhd/dot_general | solution.py:95
  143.0 14.4 %fusion.203 = f32[2,1,512,8,64]{2,4,3,1,0:T(8,128)} fusion(f32[2,1,512,8,64]{2,4,3,1,0:T(8,128)} %get-tuple-element.471, s32[]{:T(128)S(6)} %copy.169, f32[8,512,512]{1,2,0:T(8,128)} %fusion.201, f32[8,512,512]{1,2,0:T(8,128)} %copy-done, f32[8,512]{1,0:T(8,128)S(1)} %dynamic-slice_bitcast_fusion.7, ...), kind=kOutput, calls=%fused_computation.44.clone.1 | convolution fusion | flops 291508736 | bytes 35685376 | tf_op jit(solution)/shard_map/while/body/eval_jaxpr/nhqk,nkhd->nqhd/dot_general | solution.py:92
  170.4 15.7 %fusion.204 = f32[2,1,512,8,64]{2,4,3,1,0:T(8,128)} fusion(f32[2,1,512,8,64]{2,4,3,1,0:T(8,128)} %get-tuple-element.472, s32[]{:T(128)S(6)} %copy.169, f32[8,512,512]{1,2,0:T(8,128)} %fusion.201, f32[8,512,512]{1,2,0:T(8,128)} %copy-done, f32[8,512]{1,0:T(8,128)S(1)} %dynamic-slice_bitcast_fusion.7, ...), kind=kOutput, calls=%fused_computation.46.clone.1 | convolution fusion | flops 291508736 | bytes 35685376 | tf_op jit(solution)/shard_map/while/body/eval_jaxpr/nhqk,nqhd->nkhd/dot_general | solution.py:95
  186.0 14.4 %fusion.203 = f32[2,1,512,8,64]{2,4,3,1,0:T(8,128)} fusion(f32[2,1,512,8,64]{2,4,3,1,0:T(8,128)} %get-tuple-element.471, s32[]{:T(128)S(6)} %copy.169, f32[8,512,512]{1,2,0:T(8,128)} %fusion.201, f32[8,512,512]{1,2,0:T(8,128)} %copy-done, f32[8,512]{1,0:T(8,128)S(1)} %dynamic-slice_bitcast_fusion.7, ...), kind=kOutput, calls=%fused_computation.44.clone.1 | convolution fusion | flops 291508736 | bytes 35685376 | tf_op jit(solution)/shard_map/while/body/eval_jaxpr/nhqk,nkhd->nqhd/dot_general | solution.py:92
  211.5 15.6 %fusion.147 = f32[1024,2048]{1,0:T(8,128)} fusion(bf16[1024,2048]{1,0:T(8,128)(2,1)} %fusion.106, bf16[2048,2048]{1,0:T(8,128)(2,1)} %all-gather.14.cloned.1.call-done), kind=kOutput, calls=%fused_computation.179 | convolution fusion | flops 8589934592 | bytes 20971520 | tf_op jit(solution)/shard_map/dot_general | solution.py:187
  227.1 19.2 %fusion.143 = (f32[2048]{0:T(1024)S(1)}, bf16[1024,2048]{1,0:T(8,128)(2,1)S(1)}) fusion(f32[1024,2048]{1,0:T(8,128)} %fusion.147, f32[2048]{0:T(1024)S(1)} %copy-done.25, bf16[1024,2048]{1,0:T(8,128)(2,1)} %param.31, bf16[2048,2048]{1,0:T(8,128)(2,1)} %all-gather.16.cloned.1.call-done), kind=kOutput, calls=%fused_computation.176 | convolution fusion | flops 8636069888 | bytes 25182208 | tf_op jit(solution)/shard_map/dot_general | solution.py:214
  246.4 11.1 fusion.129
  257.4 12.7 %add_convert_fusion = bf16[1024,2048]{1,0:T(8,128)(2,1)} fusion(f32[1024,2048]{1,0:T(8,128)} %fusion.129, bf16[1024,1536]{0,1:T(8,128)(2,1)S(1)} %bitcast.234, bf16[2048,1536]{0,1:T(8,128)(2,1)} %bitcast.255), kind=kOutput, calls=%fused_computation.111 | convolution fusion | flops 6446645248 | bytes 22020096 | tf_op jit(solution)/shard_map/dot_general | solution.py:236
  272.7 16.4 %fusion.142 = f32[1024,2048]{1,0:T(8,128)S(1)} fusion(bf16[2048,2048]{1,0:T(8,128)(2,1)} %all-gather.16.cloned.1.call-done, f32[1024,2048]{1,0:T(8,128)} %fusion.147, f32[2048]{0:T(1024)S(1)} %copy-done.25), kind=kOutput, calls=%fused_computation.175 | convolution fusion | flops 8610906112 | bytes 25174016 | tf_op jit(solution)/shard_map/dot_general | solution.py:191
  295.0 6.5 fusion.148
  301.6 12.7 %fusion.121 = f32[2048,3,512]{2,0,1:T(8,128)} fusion(bf16[3,512,1024]{2,1,0:T(8,128)(2,1)} %bitcast.235, bf16[1024,2048]{1,0:T(8,128)(2,1)} %fusion.106), kind=kOutput, calls=%fused_computation.114 | convolution fusion | flops 6442450944 | bytes 19922944 | tf_op jit(solution)/shard_map/dot_general | solution.py:233
  314.3 17.3 %fusion.141 = f32[2048,2048]{1,0:T(8,128)} fusion(bf16[1024,2048]{1,0:T(8,128)(2,1)} %param.31, f32[1024,2048]{1,0:T(8,128)} %fusion.147, f32[2048]{0:T(1024)S(1)} %copy-done.25), kind=kOutput, calls=%fused_computation.174 | convolution fusion | flops 8610906112 | bytes 29368320 | tf_op jit(solution)/shard_map/dot_general | solution.py:208
  331.9 15.2 %fusion.127 = f32[2048,2048]{1,0:T(8,128)} fusion(bf16[1024,2048]{1,0:T(8,128)(2,1)} %fusion.106, bf16[1024,2048]{1,0:T(8,128)(2,1)} %copy-done.33), kind=kOutput, calls=%fused_computation.126 | convolution fusion | flops 8589934592 | bytes 25165824 | tf_op jit(solution)/shard_map/dot_general | solution.py:218
  350.3 8.6 all-gather.4
  358.9 8.3 all-gather.3
  370.3 54.7 %all-reduce.14.cloned.1.call-done = bf16[1024,2048]{1,0:T(8,128)(2,1)} async-done(((bf16[1024,2048]{1,0:T(8,128)(2,1)}), bf16[1024,2048]{1,0:T(8,128)(2,1)}) %all-reduce.14.cloned.1.call-update) | async-done | bytes 4194320 | tf_op jit(solution)/shard_map/psum | solution.py:241
  431.2 285.9 %all-reduce.12.cloned.1.call-done = f32[1024,2048]{1,0:T(8,128)} async-done(((f32[1024,2048]{1,0:T(8,128)}), f32[1024,2048]{1,0:T(8,128)}) %all-reduce.12.cloned.1.call-update) | async-done | bytes 8388624 | tf_op jit(solution)/shard_map/psum | solution.py:196
  717.2 13.4 %convert_reduce_fusion.2 = (f32[2048]{0:T(1024)S(1)}, f32[1024,2048]{1,0:T(8,128)}, bf16[1024,2048]{1,0:T(8,128)(2,1)}) fusion(bf16[1024,2048]{1,0:T(8,128)(2,1)} %param.31, f32[1024]{0:T(1024)S(1)} %broadcast_multiply_fusion.1, f32[1024]{0:T(1024)S(1)} %copy-done.22, bf16[1024,2048]{1,0:T(8,128)(2,1)} %param.18, f32[1024]{0:T(1024)S(1)} %broadcast_multiply_fusion.2, ...), kind=kLoop, calls=%fused_computation.89 | loop fusion | flops 33552384 | bytes 33603584 | tf_op jit(solution)/shard_map/reduce_sum | solution.py:206
  730.6 25.7 %all-reduce.8 = (f32[2048]{0:T(1024)S(1)}, f32[2048]{0:T(1024)S(1)}, f32[2,8,64]{2,1,0:T(8,128)S(1)}, f32[8,32]{0,1:T(8,128)S(1)}, f32[2048]{0:T(1024)S(1)}, /*index=5*/f32[32,64]{1,0:T(8,128)S(1)}) all-reduce(f32[2048]{0:T(1024)S(1)} %get-tuple-element.247, ...), channel_id=2, replica_groups=mesh['dp'=8,'tensor'=4] {'dp'}, use_global_device_ids=true, to_apply=%region_16.17.clone | all-reduce | flops 9472 | bytes 75776
  759.6 12.1 %reduce-scatter.9.cloned.1.call-done = f32[512,256]{1,0:T(8,128)} async-done(((f32[512,2048]{1,0:T(8,128)}), f32[512,256]{1,0:T(8,128)}) %reduce-scatter.9.cloned.1.call-update) | async-done | bytes 524304 | tf_op jit(solution)/shard_map/reduce_scatter | solution.py:260
  771.7 96.2 %reduce-scatter.7.cloned.1.call-done = f32[256,3,512]{2,0,1:T(8,128)} async-done(((f32[2048,3,512]{2,0,1:T(8,128)}), f32[256,3,512]{2,0,1:T(8,128)}) %reduce-scatter.7.cloned.1.call-update) | async-done | bytes 1572880 | tf_op jit(solution)/shard_map/reduce_scatter | solution.py:257
  867.9 120.1 %reduce-scatter.13.cloned.1.call-done = f32[2048,256]{1,0:T(8,128)} async-done(((f32[2048,2048]{1,0:T(8,128)}), f32[2048,256]{1,0:T(8,128)}) %reduce-scatter.13.cloned.1.call-update) | async-done | bytes 2097168 | tf_op jit(solution)/shard_map/reduce_scatter | solution.py:264
  988.0 120.2 %reduce-scatter.11.cloned.1.call-done = f32[256,2048]{1,0:T(8,128)} async-done(((f32[2048,2048]{1,0:T(8,128)}), f32[256,2048]{1,0:T(8,128)}) %reduce-scatter.11.cloned.1.call-update) | async-done | bytes 2097168 | tf_op jit(solution)/shard_map/reduce_scatter | solution.py:262
  (205 shorter events, 106.2 us)
Async XLA Ops:
  7.2 34.6 %copy-start.28 = (bf16[8,4]{0,1:T(4,128)(2,1)S(1)}, bf16[8,4]{0,1:T(4,128)(2,1)}, u32[]{:S(2)}) copy-start(bf16[8,4]{0,1:T(4,128)(2,1)} %param.24) | copy-start | bytes 196
  7.2 42.6 %copy-start.27 = (bf16[32,8]{0,1:T(8,128)(2,1)S(1)}, bf16[32,8]{0,1:T(8,128)(2,1)}, u32[]{:S(2)}) copy-start(bf16[32,8]{0,1:T(8,128)(2,1)} %param.28) | copy-start | bytes 1540
  7.2 67.5 %all-gather.12.cloned.1.call-start = ((), (), s32[]{:S(2)}) async-start(), calls=%async_computation.5 | async-start | bytes 2359296 | tf_op jit(solution)/shard_map/all_gather | solution.py:123
  7.9 81.4 %all-gather.10.cloned.1.call-start = ((), (), s32[]{:S(2)}) async-start(), calls=%async_computation.4 | async-start | bytes 7077888 | tf_op jit(solution)/shard_map/all_gather | solution.py:120
  10.3 201.2 %all-gather.14.cloned.1.call-start = ((), (), s32[]{:S(2)}) async-start(), calls=%async_computation.6 | async-start | bytes 9437184 | tf_op jit(solution)/shard_map/all_gather | solution.py:125
  11.0 216.1 %all-gather.16.cloned.1.call-start = ((), (), s32[]{:S(2)}) async-start(), calls=%async_computation.7 | async-start | bytes 9437184 | tf_op jit(solution)/shard_map/all_gather | solution.py:127
  11.6 413.4 %all-reduce.14.cloned.1.call-start = ((), (), s32[]{:S(2)}) async-start(), calls=%async_computation.9 | async-start | bytes 8388608 | tf_op jit(solution)/shard_map/psum | solution.py:241
  18.7 62.2 %copy-start.21 = (f32[1024]{0:T(1024)}, f32[1024]{0:T(1024)S(1)}, u32[]{:S(2)}) copy-start(f32[1024]{0:T(1024)S(1)} %broadcast_multiply_fusion.3) | copy-start | bytes 12292
  22.2 58.6 %copy-start.23 = (f32[1024]{0:T(1024)}, f32[1024]{0:T(1024)S(1)}, u32[]{:S(2)}) copy-start(f32[1024]{0:T(1024)S(1)} %add_rsqrt_fusion) | copy-start | bytes 12292
  41.7 39.1 %copy-start.19 = (f32[8,1,256]{2,1,0:T(1,128)}, f32[8,1,256]{2,1,0:T(1,128)S(1)}, u32[]{:S(2)}) copy-start(f32[8,1,256]{2,1,0:T(1,128)S(1)} %convert_element_type.142) | copy-start | bytes 24580
  115.0 88.3 %copy-start.18 = (f32[2,512,16]{1,2,0:T(8,128)S(1)}, f32[2,512,16]{1,2,0:T(8,128)}, u32[]{:S(2)}) copy-start(f32[2,512,16]{1,2,0:T(8,128)} %get-tuple-element.316) | copy-start | bytes 196612
  115.0 5.1 copy-start.1
  115.0 5.1 copy-start.6
  115.1 8.7 copy-start.3
  157.5 8.2 copy-start.3
  200.6 6.3 copy-start.8
  211.5 45.9 %copy-start.14 = (bf16[192,8,2,512]{3,1,2,0:T(8,128)(2,1)}, bf16[192,8,2,512]{3,1,2,0:T(8,128)(2,1)S(1)}, u32[]{:S(2)}) copy-start(bf16[192,8,2,512]{3,1,2,0:T(8,128)(2,1)S(1)} %copy.149) | copy-start | bytes 9437188
  211.5 15.6 %copy-start.25 = (f32[2048]{0:T(1024)S(1)}, f32[2048]{0:T(1024)}, u32[]{:S(2)}) copy-start(f32[2048]{0:T(1024)} %reshape.385) | copy-start | bytes 24580
  227.1 19.2 %copy-start.29 = (bf16[2048,2048]{1,0:T(8,128)(2,1)S(1)}, bf16[2048,2048]{1,0:T(8,128)(2,1)}, u32[]{:S(2)}) copy-start(bf16[2048,2048]{1,0:T(8,128)(2,1)} %all-gather.14.cloned.1.call-done) | copy-start | bytes 25165828
  246.3 11.1 copy-start.33
  270.1 447.1 %all-reduce.12.cloned.1.call-start = ((), (), s32[]{:S(2)}) async-start(), calls=%async_computation.8 | async-start | bytes 16777216 | tf_op jit(solution)/shard_map/psum | solution.py:196
  272.7 16.4 %copy-start.15 = (bf16[512,2048]{1,0:T(8,128)(2,1)S(1)}, bf16[512,2048]{1,0:T(8,128)(2,1)}, u32[]{:S(2)}) copy-start(bf16[512,2048]{1,0:T(8,128)(2,1)} %all-gather.12.cloned.1.call-done) | copy-start | bytes 6291460
  294.8 476.9 %reduce-scatter.9.cloned.1.call-start = ((), (), s32[]{:S(2)}) async-start(), calls=%async_computation.11 | async-start | bytes 4718592 | tf_op jit(solution)/shard_map/reduce_scatter | solution.py:260
  301.5 566.4 %reduce-scatter.7.cloned.1.call-start = ((), (), s32[]{:S(2)}) async-start(), calls=%async_computation.10 | async-start | bytes 14155776 | tf_op jit(solution)/shard_map/reduce_scatter | solution.py:257
  314.2 673.8 %reduce-scatter.13.cloned.1.call-start = ((), (), s32[]{:S(2)}) async-start(), calls=%async_computation.13 | async-start | bytes 18874368 | tf_op jit(solution)/shard_map/reduce_scatter | solution.py:264
  331.6 776.7 %reduce-scatter.11.cloned.1.call-start = ((), (), s32[]{:S(2)}) async-start(), calls=%async_computation.12 | async-start | bytes 18874368 | tf_op jit(solution)/shard_map/reduce_scatter | solution.py:262
  347.1 20.1 %copy-start.9 = (f32[2,1,512,8,64]{2,4,3,1,0:T(8,128)S(1)}, f32[2,1,512,8,64]{2,4,3,1,0:T(8,128)}, u32[]{:S(2)}) copy-start(f32[2,1,512,8,64]{2,4,3,1,0:T(8,128)} %get-tuple-element.109) | copy-start | bytes 6291460
  347.1 21.7 %copy-start.5 = (f32[2,512,8,32]{1,3,2,0:T(8,128)S(1)}, f32[2,512,8,32]{1,3,2,0:T(8,128)}, u32[]{:S(2)}) copy-start(f32[2,512,8,32]{1,3,2,0:T(8,128)} %copy-done.4) | copy-start | bytes 3145732
  347.1 77.9 %copy-start.20 = (f32[8,1,256]{2,1,0:T(1,128)S(1)}, f32[8,1,256]{2,1,0:T(1,128)}, u32[]{:S(2)}) copy-start(f32[8,1,256]{2,1,0:T(1,128)} %copy-done.19) | copy-start | bytes 24580
  347.1 77.9 %copy-start.22 = (f32[1024]{0:T(1024)S(1)}, f32[1024]{0:T(1024)}, u32[]{:S(2)}) copy-start(f32[1024]{0:T(1024)} %copy-done.21) | copy-start | bytes 12292
  347.1 77.9 %copy-start.24 = (f32[1024]{0:T(1024)S(1)}, f32[1024]{0:T(1024)}, u32[]{:S(2)}) copy-start(f32[1024]{0:T(1024)} %copy-done.23) | copy-start | bytes 12292
  757.0 351.8 %copy-start.26 = (f32[256]{0:T(256)}, f32[256]{0:T(256)S(1)}, u32[]{:S(2)}) copy-start(f32[256]{0:T(256)S(1)} %dynamic-slice.9) | copy-start | bytes 3076
  (20 other events, 47.7 us)
Sparse Core Ops, SparseCore 0:
  9.9 30.8 all-gather.11
  42.6 46.6 all-gather.9
  91.2 54.2 all-gather.13
  147.2 55.8 all-gather.15
  270.2 154.7 all-reduce.13
  427.3 289.7 all-reduce.11
  721.1 50.5 reduce-scatter.8
  775.7 92.0 reduce-scatter.6
  872.0 115.9 reduce-scatter.12
  992.0 116.2 reduce-scatter.10
where the time goes:
time: 1120 us
  waiting for transfers between devices  695 us (62%)
  matrix products  232 us (21%)
  blocking collectives  87.8 us (8%)
  other arithmetic  44.5 us (4%)
  local copies, waits for them, and re-layouts  39 us (3%)
  between operations  17.1 us (2%)
    psum x1, waiting for transfers between devices, local(): summed_out = lax.psum(branches, 'tensor')  286 us
    reduce_scatter x1, waiting for transfers between devices, local(): lax.psum_scatter(grad_up, 'dp', scatter_dimension=0, tiled=True)  120 us
    reduce_scatter x1, waiting for transfers between devices, local(): lax.psum_scatter(grad_down, 'dp', scatter_dimension=1, tiled=True)  120 us
    reduce_scatter x1, waiting for transfers between devices, local(): lax.psum_scatter(grad_qkv, 'dp', scatter_dimension=0, tiled=True)  96.2 us
    psum x1, waiting for transfers between devices, local(): lax.psum(grad_normed_part.astype(jnp.bfloat16), 'tensor')  54.7 us
    dot_general x2, matrix products, attend_back_group(): jnp.einsum('nhqk,nqhd->nkhd', grad_scores, queries, preferred_element_typ...  30.2 us
    dot_general x2, matrix products, attend_back_group(): jnp.einsum('nhqk,nkhd->nqhd', grad_scores, key_rows, preferred_element_ty...  28.8 us
    unnamed x1, blocking collectives  25.7 us
  transfers between devices with their start and end apart: 10, of which 7 were waited for; matrix products, arithmetic and copies ran while one was open for 23% of the time, Pallas kernels for 0%

commit v1 on v0

--- a/solution.py
+++ b/solution.py
@@ -193,7 +193,8 @@
     )
     dense_shift = dense_shift_all.astype(jnp.float32)
     down_shift = down_shift_all.astype(jnp.float32)
-    summed_out = lax.psum(branches, "tensor")
+    parts = lax.all_gather(branches, "tensor", axis=0, tiled=False)
+    summed_out = parts.sum(axis=0)
     block_output = (widened + summed_out + dense_shift + down_shift).astype(jnp.bfloat16)
     gain_back, qkv_back, dense_back, up_back, down_back = (
         lax.all_gather(norm_gain, "dp", axis=0, tiled=True),

time: 1120 us -> 1390 us (1.24)
  waiting for transfers between devices: 695 us -> 947 us
  other arithmetic: 44.5 us -> 61.5 us
    all_gather x0 -> x1, waiting for transfers between devices: none -> 556 us  [local(): parts = lax.all_gather(branches, 'tensor', axis=0, tiled=False)]
    psum x1 -> x0, waiting for transfers between devices: 286 us -> none  [local(): summed_out = lax.psum(branches, 'tensor')]
    reduce_sum x0 -> x1, other arithmetic: none -> 17.1 us  [local(): summed_out = parts.sum(axis=0)]
  transfers between devices with their start and end apart: 10 -> 10, of which waited for: 7 -> 6; matrix products, arithmetic and copies ran while one was open for 23% -> 20% of each run, Pallas kernels for 0% -> 0%
where the time goes in v1:
time: 1390 us; the launch traced here: 1380 us
  waiting for transfers between devices  947 us (68%)
  matrix products  231 us (17%)
  blocking collectives  87 us (6%)
  other arithmetic  61.5 us (4%)
  local copies, waits for them, and re-layouts  39 us (3%)
  between operations  16.9 us (1%)
    all_gather x1, waiting for transfers between devices, local(): parts = lax.all_gather(branches, 'tensor', axis=0, tiled=False)  556 us
    reduce_scatter x1, waiting for transfers between devices, local(): lax.psum_scatter(grad_up, 'dp', scatter_dimension=0, tiled=True)  120 us
    reduce_scatter x1, waiting for transfers between devices, local(): lax.psum_scatter(grad_down, 'dp', scatter_dimension=1, tiled=True)  120 us
    reduce_scatter x1, waiting for transfers between devices, local(): lax.psum_scatter(grad_qkv, 'dp', scatter_dimension=0, tiled=True)  91.1 us
    psum x1, waiting for transfers between devices, local(): lax.psum(grad_normed_part.astype(jnp.bfloat16), 'tensor')  54.4 us
    dot_general x2, matrix products, attend_back_group(): jnp.einsum('nhqk,nqhd->nkhd', grad_scores, queries, preferred_element_typ...  30.2 us
    dot_general x2, matrix products, attend_back_group(): jnp.einsum('nhqk,nkhd->nqhd', grad_scores, key_rows, preferred_element_ty...  28.8 us
  transfers between devices with their start and end apart: 10, of which 6 were waited for; matrix products, arithmetic and copies ran while one was open for 20% of the time, Pallas kernels for 0%

profile of v1, /device:TPU:0, one launch (start us, length us, event | category | flops | bytes accessed | tf_op | source)
XLA Modules:
  0.0 1384.7 jit_solution(2574425530127385075)
XLA Ops:
  22.3 10.4 all-gather.2
  32.7 9.1 all-gather.1
  41.8 8.0 all-gather.3
  49.8 9.2 all_gather.51
  59.8 8.3 all_gather.47
  89.3 10.1 fusion.146
  101.6 13.5 while.26
  115.1 85.7 %while.27 = (s32[]{:T(128)}, f32[2,1,512,8,64]{2,4,3,1,0:T(8,128)}, f32[2,1,512,8,64]{2,4,3,1,0:T(8,128)}, f32[2,1,512,8,64]{2,4,3,1,0:T(8,128)}, bf16[2,1,512,8...) while((s32[]{:T(128)}, f32[2,1,512,8,64]{2,4,3,1,0:T(8,128)}, ...), condition=%wide.region_11.12_spmd, body=%wide.region_9.11_spmd.sunk | while | flops 1396712448 | bytes 159765776 | solution.py:221
  128.5 14.5 %fusion.204 = f32[2,1,512,8,64]{2,4,3,1,0:T(8,128)} fusion(f32[2,1,512,8,64]{2,4,3,1,0:T(8,128)} %get-tuple-element.472, s32[]{:T(128)S(6)} %copy.169, f32[8,512,512]{1,2,0:T(8,128)} %fusion.201, f32[8,512,512]{1,2,0:T(8,128)} %copy-done, f32[8,512]{1,0:T(8,128)S(1)} %dynamic-slice_bitcast_fusion.7, ...), kind=kOutput, calls=%fused_computation.46.clone.1 | convolution fusion | flops 291508736 | bytes 35685376 | tf_op jit(solution)/shard_map/while/body/eval_jaxpr/nhqk,nqhd->nkhd/dot_general | solution.py:95
  143.1 14.4 %fusion.203 = f32[2,1,512,8,64]{2,4,3,1,0:T(8,128)} fusion(f32[2,1,512,8,64]{2,4,3,1,0:T(8,128)} %get-tuple-element.471, s32[]{:T(128)S(6)} %copy.169, f32[8,512,512]{1,2,0:T(8,128)} %fusion.201, f32[8,512,512]{1,2,0:T(8,128)} %copy-done, f32[8,512]{1,0:T(8,128)S(1)} %dynamic-slice_bitcast_fusion.7, ...), kind=kOutput, calls=%fused_computation.44.clone.1 | convolution fusion | flops 291508736 | bytes 35685376 | tf_op jit(solution)/shard_map/while/body/eval_jaxpr/nhqk,nkhd->nqhd/dot_general | solution.py:92
  170.4 15.7 %fusion.204 = f32[2,1,512,8,64]{2,4,3,1,0:T(8,128)} fusion(f32[2,1,512,8,64]{2,4,3,1,0:T(8,128)} %get-tuple-element.472, s32[]{:T(128)S(6)} %copy.169, f32[8,512,512]{1,2,0:T(8,128)} %fusion.201, f32[8,512,512]{1,2,0:T(8,128)} %copy-done, f32[8,512]{1,0:T(8,128)S(1)} %dynamic-slice_bitcast_fusion.7, ...), kind=kOutput, calls=%fused_computation.46.clone.1 | convolution fusion | flops 291508736 | bytes 35685376 | tf_op jit(solution)/shard_map/while/body/eval_jaxpr/nhqk,nqhd->nkhd/dot_general | solution.py:95
  186.1 14.4 %fusion.203 = f32[2,1,512,8,64]{2,4,3,1,0:T(8,128)} fusion(f32[2,1,512,8,64]{2,4,3,1,0:T(8,128)} %get-tuple-element.471, s32[]{:T(128)S(6)} %copy.169, f32[8,512,512]{1,2,0:T(8,128)} %fusion.201, f32[8,512,512]{1,2,0:T(8,128)} %copy-done, f32[8,512]{1,0:T(8,128)S(1)} %dynamic-slice_bitcast_fusion.7, ...), kind=kOutput, calls=%fused_computation.44.clone.1 | convolution fusion | flops 291508736 | bytes 35685376 | tf_op jit(solution)/shard_map/while/body/eval_jaxpr/nhqk,nkhd->nqhd/dot_general | solution.py:92
  211.8 15.6 %fusion.147 = f32[1024,2048]{1,0:T(8,128)} fusion(bf16[1024,2048]{1,0:T(8,128)(2,1)} %fusion.106, bf16[2048,2048]{1,0:T(8,128)(2,1)} %all-gather.16.cloned.1.call-done), kind=kOutput, calls=%fused_computation.179 | convolution fusion | flops 8589934592 | bytes 20971520 | tf_op jit(solution)/shard_map/dot_general | solution.py:187
  227.3 18.9 %fusion.143 = (f32[2048]{0:T(1024)S(1)}, bf16[1024,2048]{1,0:T(8,128)(2,1)S(1)}) fusion(f32[1024,2048]{1,0:T(8,128)} %fusion.147, f32[2048]{0:T(1024)S(1)} %copy-done.25, bf16[1024,2048]{1,0:T(8,128)(2,1)} %param.31, bf16[2048,2048]{1,0:T(8,128)(2,1)} %all-gather.18.cloned.1.call-done), kind=kOutput, calls=%fused_computation.176 | convolution fusion | flops 8636069888 | bytes 25182208 | tf_op jit(solution)/shard_map/dot_general | solution.py:215
  246.3 11.1 fusion.129
  257.4 12.7 add_convert_fusion
  272.7 16.4 %fusion.142 = f32[1024,2048]{1,0:T(8,128)S(1)} fusion(bf16[2048,2048]{1,0:T(8,128)(2,1)} %all-gather.18.cloned.1.call-done, f32[1024,2048]{1,0:T(8,128)} %fusion.147, f32[2048]{0:T(1024)S(1)} %copy-done.25), kind=kOutput, calls=%fused_computation.175 | convolution fusion | flops 8610906112 | bytes 25174016 | tf_op jit(solution)/shard_map/dot_general | solution.py:191
  295.2 6.5 fusion.148
  301.8 12.6 fusion.121
  314.6 17.2 %fusion.141 = f32[2048,2048]{1,0:T(8,128)} fusion(bf16[1024,2048]{1,0:T(8,128)(2,1)} %param.31, f32[1024,2048]{1,0:T(8,128)} %fusion.147, f32[2048]{0:T(1024)S(1)} %copy-done.25), kind=kOutput, calls=%fused_computation.174 | convolution fusion | flops 8610906112 | bytes 29368320 | tf_op jit(solution)/shard_map/dot_general | solution.py:209
  332.1 15.2 %fusion.127 = f32[2048,2048]{1,0:T(8,128)} fusion(bf16[1024,2048]{1,0:T(8,128)(2,1)} %fusion.106, bf16[1024,2048]{1,0:T(8,128)(2,1)} %copy-done.33), kind=kOutput, calls=%fused_computation.126 | convolution fusion | flops 8589934592 | bytes 25165824 | tf_op jit(solution)/shard_map/dot_general | solution.py:219
  350.5 8.5 all-gather.5
  359.0 8.4 all-gather.4
  370.5 54.4 %all-reduce.11.cloned.1.call-done = bf16[1024,2048]{1,0:T(8,128)(2,1)} async-done(((bf16[1024,2048]{1,0:T(8,128)(2,1)}), bf16[1024,2048]{1,0:T(8,128)(2,1)}) %all-reduce.11.cloned.1.call-update) | async-done | bytes 4194320 | tf_op jit(solution)/shard_map/psum | solution.py:242
  424.8 6.2 fusion.120
  431.1 555.6 %all-gather.20.cloned.1.call-done = f32[4096,2048]{1,0:T(8,128)} async-done(((f32[1024,2048]{1,0:T(8,128)}), f32[4096,2048]{1,0:T(8,128)}) %all-gather.20.cloned.1.call-update) | async-done | bytes 33554448 | tf_op jit(solution)/shard_map/all_gather | solution.py:196
  986.6 17.1 %reduce_sum.128 = f32[1024,2048]{1,0:T(8,128)} reduce(f32[4,1024,2048]{2,1,0:T(8,128)} %bitcast.229, f32[]{:T(128)} %constant.72.clone.1), dimensions={0}, to_apply=%region_8.9 | reduce | flops 6291456 | bytes 41943044 | tf_op jit(solution)/shard_map/reduce_sum | solution.py:197
  1003.7 13.3 convert_reduce_fusion.2
  1017.0 25.3 %all-reduce.8 = (f32[2048]{0:T(1024)S(1)}, f32[2048]{0:T(1024)S(1)}, f32[2,8,64]{2,1,0:T(8,128)S(1)}, f32[8,32]{0,1:T(8,128)S(1)}, f32[2048]{0:T(1024)S(1)}, /*index=5*/f32[32,64]{1,0:T(8,128)S(1)}) all-reduce(f32[2048]{0:T(1024)S(1)} %get-tuple-element.247, ...), channel_id=3, replica_groups=mesh['dp'=8,'tensor'=4] {'dp'}, use_global_device_ids=true, to_apply=%region_16.17.clone | all-reduce | flops 9472 | bytes 75776
  1045.6 91.1 %reduce-scatter.7.cloned.1.call-done = f32[256,3,512]{2,0,1:T(8,128)} async-done(((f32[2048,3,512]{2,0,1:T(8,128)}), f32[256,3,512]{2,0,1:T(8,128)}) %reduce-scatter.7.cloned.1.call-update) | async-done | bytes 1572880 | tf_op jit(solution)/shard_map/reduce_scatter | solution.py:258
  1136.7 120.2 %reduce-scatter.13.cloned.1.call-done = f32[2048,256]{1,0:T(8,128)} async-done(((f32[2048,2048]{1,0:T(8,128)}), f32[2048,256]{1,0:T(8,128)}) %reduce-scatter.13.cloned.1.call-update) | async-done | bytes 2097168 | tf_op jit(solution)/shard_map/reduce_scatter | solution.py:265
  1256.9 120.2 %reduce-scatter.11.cloned.1.call-done = f32[256,2048]{1,0:T(8,128)} async-done(((f32[2048,2048]{1,0:T(8,128)}), f32[256,2048]{1,0:T(8,128)}) %reduce-scatter.11.cloned.1.call-update) | async-done | bytes 2097168 | tf_op jit(solution)/shard_map/reduce_scatter | solution.py:263
  (206 shorter events, 106.7 us)
Async XLA Ops:
  7.2 34.6 %copy-start.28 = (bf16[8,4]{0,1:T(4,128)(2,1)S(1)}, bf16[8,4]{0,1:T(4,128)(2,1)}, u32[]{:S(2)}) copy-start(bf16[8,4]{0,1:T(4,128)(2,1)} %param.24) | copy-start | bytes 196
  7.2 42.6 %copy-start.27 = (bf16[32,8]{0,1:T(8,128)(2,1)S(1)}, bf16[32,8]{0,1:T(8,128)(2,1)}, u32[]{:S(2)}) copy-start(bf16[32,8]{0,1:T(8,128)(2,1)} %param.28) | copy-start | bytes 1540
  7.2 67.2 %all-gather.14.cloned.1.call-start = ((), (), s32[]{:S(2)}) async-start(), calls=%async_computation.5 | async-start | bytes 2359296 | tf_op jit(solution)/shard_map/all_gather | solution.py:123
  7.9 81.4 %all-gather.12.cloned.1.call-start = ((), (), s32[]{:S(2)}) async-start(), calls=%async_computation.4 | async-start | bytes 7077888 | tf_op jit(solution)/shard_map/all_gather | solution.py:120
  10.3 201.5 %all-gather.16.cloned.1.call-start = ((), (), s32[]{:S(2)}) async-start(), calls=%async_computation.6 | async-start | bytes 9437184 | tf_op jit(solution)/shard_map/all_gather | solution.py:125
  11.0 216.3 %all-gather.18.cloned.1.call-start = ((), (), s32[]{:S(2)}) async-start(), calls=%async_computation.7 | async-start | bytes 9437184 | tf_op jit(solution)/shard_map/all_gather | solution.py:127
  11.6 413.2 %all-reduce.11.cloned.1.call-start = ((), (), s32[]{:S(2)}) async-start(), calls=%async_computation.8 | async-start | bytes 8388608 | tf_op jit(solution)/shard_map/psum | solution.py:242
  18.7 61.9 %copy-start.21 = (f32[1024]{0:T(1024)}, f32[1024]{0:T(1024)S(1)}, u32[]{:S(2)}) copy-start(f32[1024]{0:T(1024)S(1)} %broadcast_multiply_fusion.3) | copy-start | bytes 12292
  22.3 58.3 %copy-start.23 = (f32[1024]{0:T(1024)}, f32[1024]{0:T(1024)S(1)}, u32[]{:S(2)}) copy-start(f32[1024]{0:T(1024)S(1)} %add_rsqrt_fusion) | copy-start | bytes 12292
  41.8 38.8 %copy-start.19 = (f32[8,1,256]{2,1,0:T(1,128)}, f32[8,1,256]{2,1,0:T(1,128)S(1)}, u32[]{:S(2)}) copy-start(f32[8,1,256]{2,1,0:T(1,128)S(1)} %convert_element_type.142) | copy-start | bytes 24580
  115.1 88.5 %copy-start.18 = (f32[2,512,16]{1,2,0:T(8,128)S(1)}, f32[2,512,16]{1,2,0:T(8,128)}, u32[]{:S(2)}) copy-start(f32[2,512,16]{1,2,0:T(8,128)} %get-tuple-element.316) | copy-start | bytes 196612
  115.1 5.2 copy-start.1
  115.1 5.2 copy-start.6
  115.1 8.7 copy-start.3
  157.5 8.1 copy-start.3
  200.8 6.3 copy-start.8
  211.7 45.6 %copy-start.14 = (bf16[192,8,2,512]{3,1,2,0:T(8,128)(2,1)}, bf16[192,8,2,512]{3,1,2,0:T(8,128)(2,1)S(1)}, u32[]{:S(2)}) copy-start(bf16[192,8,2,512]{3,1,2,0:T(8,128)(2,1)S(1)} %copy.149) | copy-start | bytes 9437188
  211.7 15.6 %copy-start.25 = (f32[2048]{0:T(1024)S(1)}, f32[2048]{0:T(1024)}, u32[]{:S(2)}) copy-start(f32[2048]{0:T(1024)} %reshape.385) | copy-start | bytes 24580
  227.3 19.0 %copy-start.29 = (bf16[2048,2048]{1,0:T(8,128)(2,1)S(1)}, bf16[2048,2048]{1,0:T(8,128)(2,1)}, u32[]{:S(2)}) copy-start(bf16[2048,2048]{1,0:T(8,128)(2,1)} %all-gather.16.cloned.1.call-done) | copy-start | bytes 25165828
  246.3 11.1 copy-start.33
  270.1 716.6 %all-gather.20.cloned.1.call-start = ((), (), s32[]{:S(2)}) async-start(), calls=%async_computation.13 | async-start | bytes 41943040 | tf_op jit(solution)/shard_map/all_gather | solution.py:196
  272.7 16.4 %copy-start.15 = (bf16[512,2048]{1,0:T(8,128)(2,1)S(1)}, bf16[512,2048]{1,0:T(8,128)(2,1)}, u32[]{:S(2)}) copy-start(bf16[512,2048]{1,0:T(8,128)(2,1)} %all-gather.14.cloned.1.call-done) | copy-start | bytes 6291460
  294.8 750.8 %reduce-scatter.9.cloned.1.call-start = ((), (), s32[]{:S(2)}) async-start(), calls=%async_computation.10 | async-start | bytes 4718592 | tf_op jit(solution)/shard_map/reduce_scatter | solution.py:261
  301.8 834.9 %reduce-scatter.7.cloned.1.call-start = ((), (), s32[]{:S(2)}) async-start(), calls=%async_computation.9 | async-start | bytes 14155776 | tf_op jit(solution)/shard_map/reduce_scatter | solution.py:258
  314.5 942.4 %reduce-scatter.13.cloned.1.call-start = ((), (), s32[]{:S(2)}) async-start(), calls=%async_computation.12 | async-start | bytes 18874368 | tf_op jit(solution)/shard_map/reduce_scatter | solution.py:265
  331.8 1045.3 %reduce-scatter.11.cloned.1.call-start = ((), (), s32[]{:S(2)}) async-start(), calls=%async_computation.11 | async-start | bytes 18874368 | tf_op jit(solution)/shard_map/reduce_scatter | solution.py:263
  347.3 20.1 %copy-start.9 = (f32[2,1,512,8,64]{2,4,3,1,0:T(8,128)S(1)}, f32[2,1,512,8,64]{2,4,3,1,0:T(8,128)}, u32[]{:S(2)}) copy-start(f32[2,1,512,8,64]{2,4,3,1,0:T(8,128)} %get-tuple-element.109) | copy-start | bytes 6291460
  347.3 21.7 %copy-start.5 = (f32[2,512,8,32]{1,3,2,0:T(8,128)S(1)}, f32[2,512,8,32]{1,3,2,0:T(8,128)}, u32[]{:S(2)}) copy-start(f32[2,512,8,32]{1,3,2,0:T(8,128)} %copy-done.4) | copy-start | bytes 3145732
  347.3 77.5 %copy-start.20 = (f32[8,1,256]{2,1,0:T(1,128)S(1)}, f32[8,1,256]{2,1,0:T(1,128)}, u32[]{:S(2)}) copy-start(f32[8,1,256]{2,1,0:T(1,128)} %copy-done.19) | copy-start | bytes 24580
  347.3 77.5 %copy-start.22 = (f32[1024]{0:T(1024)S(1)}, f32[1024]{0:T(1024)}, u32[]{:S(2)}) copy-start(f32[1024]{0:T(1024)} %copy-done.21) | copy-start | bytes 12292
  347.3 77.5 %copy-start.24 = (f32[1024]{0:T(1024)S(1)}, f32[1024]{0:T(1024)}, u32[]{:S(2)}) copy-start(f32[1024]{0:T(1024)} %copy-done.23) | copy-start | bytes 12292
  1043.0 334.7 %copy-start.26 = (f32[256]{0:T(256)}, f32[256]{0:T(256)S(1)}, u32[]{:S(2)}) copy-start(f32[256]{0:T(256)S(1)} %dynamic-slice.9) | copy-start | bytes 3076
  (20 other events, 47.7 us)
Sparse Core Ops, SparseCore 0:
  9.9 30.8 all-gather.13
  42.6 46.6 all-gather.11
  91.2 54.2 all-gather.15
  147.2 55.8 all-gather.17
  270.2 154.5 all-reduce.10
  426.3 560.3 all-gather.19
  990.6 50.0 reduce-scatter.8
  1044.7 91.9 reduce-scatter.6
  1140.9 115.9 reduce-scatter.12
  1260.9 116.1 reduce-scatter.10
